TPU v7x, 32 devices: a whole 2x2x4 slice. The times are simulated.
32 devices in a mesh: rows: 8 (over z, y), cols: 4 (over x, core).
Axes of the slice: x: 2, y: 2, z: 4, core: 2. Of those that a mesh axis runs over, the one named last changes fastest.
Arguments:
- projector_matrix: float32 [8192, 4096], P('rows', 'cols'), may hold values from -0.0625 to 0.0625
- start_state: float32 [128, 4096], P(None, 'cols'), may hold values from -6 to 6
- decay_rate: float32 [4096], P('cols'), may hold values from 0.05 to 0.95
- escape_heat_factor: float32 [8192], P('rows'), may hold values from 0.1 to 1
- tile_block: int32 [64], P('rows'), may hold values from 0 to 63, as said below
- block_owner: int32 [64], replicated, may hold values from 0 to 7, as said below
- owner_power: float32 [4, 128, 64], P(None, None, 'rows'), may hold values from 0.2 to 5
Outputs:
- final_state: float32 [128, 4096], P(None, 'cols')
- node_temps: float32 [128, 8192], P('cols', 'rows')
- block_history: float32 [4, 128, 64], P(None, 'cols', 'rows')
Inputs may be any that keep to these rules, and one draw needn't show every extreme that they name: `block_owner`: every rows index owns exactly 8 blocks. `tile_block`: each block is named by exactly one tile.
All inputs are finite; a program needn't handle non-finite values.
Results may differ from a plain program's by a relative error of at most 0.0001.
Values sent between devices are 32-bit elements; how exact they have to be, the bound alone decides.
A program may use at most 64 MiB of HBM per device.

v0:
```python
import jax
import jax.numpy as jnp
from jax import lax
from jax.sharding import PartitionSpec as P

STEPS = 4
PATCH_POINTS = 128


escape_heat_derivative = 2.0
dominant_spectral_direction = lax.Precision.HIGHEST


def floor_positions(block_owner, per_owner):
    indices = jnp.arange(block_owner.shape[0], dtype=jnp.int32)
    same_owner = (block_owner[:, None] == block_owner[None, :]) & (
        indices[None, :] < indices[:, None]
    )
    return block_owner * per_owner + jnp.sum(same_owner.astype(jnp.int32), axis=1)


def shards(
    projector_matrix,
    start_state,
    decay_rate,
    escape_heat_factor,
    tile_block,
    block_owner,
    owner_power,
):
    node_rows = projector_matrix.shape[0]
    scen_total = start_state.shape[0]
    scen_share = scen_total // lax.axis_size("cols")
    share_start = lax.axis_index("cols") * scen_share
    tiles_here = tile_block.shape[0]
    positions = floor_positions(block_owner, tiles_here)
    tile_position = jnp.take(positions, tile_block)
    columns = jnp.arange(block_owner.shape[0], dtype=jnp.int32)
    tile_onehot = (tile_position[:, None] == columns[None, :]).astype(jnp.float32)
    all_power = lax.all_gather(owner_power, "rows", axis=2, tiled=True)
    compact_vector = start_state
    march_history = []
    own_temp = jnp.zeros((scen_share, node_rows), jnp.float32)
    for step_index in range(STEPS):
        current = compact_vector
        own_temp = lax.psum_scatter(
            jnp.einsum(
                "ec,wc->ew", current, projector_matrix, precision=dominant_spectral_direction
            ),
            "cols",
            scatter_dimension=0,
            tiled=True,
        )
        patch_mean_level = jnp.sum(
            own_temp.reshape(scen_share, tiles_here, PATCH_POINTS), axis=2
        ) * (1.0 / PATCH_POINTS)
        partial_block = jnp.dot(
            patch_mean_level, tile_onehot, precision=dominant_spectral_direction
        )
        march_history.append(partial_block)
        step_power = all_power[step_index]
        work_power = lax.dynamic_slice_in_dim(step_power, share_start, scen_share, 0)
        heating_at_patches = jnp.einsum(
            "sb,tb->st", work_power, tile_onehot, precision=dominant_spectral_direction
        )
        scen_rows = work_power.shape[0]
        spread_power = jnp.broadcast_to(
            heating_at_patches[:, :, None], (scen_rows, tiles_here, PATCH_POINTS)
        ).reshape(scen_rows, node_rows)
        heating_at_points = spread_power + escape_heat_factor[None, :] * (
            1.0 + jnp.tanh(escape_heat_derivative * own_temp)
        )
        driven_part = jnp.dot(
            lax.all_gather(heating_at_points, "cols", axis=0, tiled=True),
            projector_matrix,
            precision=dominant_spectral_direction,
        )
        driven = lax.psum(driven_part, "rows")
        compact_vector = decay_rate * current + (1.0 - decay_rate) * driven
    block_history = lax.psum_scatter(
        jnp.stack(march_history), "rows", scatter_dimension=2, tiled=True
    )
    return (compact_vector, own_temp, block_history)


def solution(mesh):
    placed = (
        P("rows", "cols"),
        P(None, "cols"),
        P("cols"),
        P("rows"),
        P("rows"),
        P(),
        P(None, None, "rows"),
    )
    return jax.shard_map(
        shards,
        mesh=mesh,
        in_specs=placed,
        out_specs=(P(None, "cols"), P("cols", "rows"), P(None, "cols", "rows")),
        check_vma=False,
    )
```

profile of v0, /device:TPU:0, one launch (start us, length us, event | category | flops | bytes accessed | tf_op | source)
XLA Modules:
  0.0 490.7 jit_solution(1599836047265483097)
XLA Ops:
  7.3 7.5 %fusion.40 = f32[128,1024]{1,0:T(8,128)} fusion(f32[128,1024]{1,0:T(8,128)} %param.8, f32[1024,1024]{1,0:T(8,128)} %param.7), kind=kOutput, calls=%fused_computation.63 | convolution fusion | flops 1610612736 | bytes 5242880 | tf_op jit(solution)/shard_map/ec,wc->ew/dot_general | solution.py:47
  15.8 32.3 %all_gather.15 = f32[4,128,64]{1,2,0:T(8,128)S(1)} all-gather(f32[4,128,8]{1,2,0:T(8,128)S(1)} %copy-done.9), channel_id=1, replica_groups=mesh['rows'=8,'cols'=4] {'rows'}, dimensions={2}, use_global_device_ids=true | all-gather | bytes 147456 | tf_op jit(solution)/shard_map/all_gather | solution.py:40
  49.5 7.2 %all_gather.16 = f32[128,1024]{1,0:T(8,128)S(1)} all-gather(f32[32,1024]{1,0:T(8,128)S(1)} %bitcast_add_fusion.3), channel_id=1, replica_groups=mesh['rows'=8,'cols'=4] {'cols'}, dimensions={0}, use_global_device_ids=true | all-gather | bytes 655360 | tf_op jit(solution)/shard_map/all_gather | solution.py:74
  56.6 5.4 %fusion.41 = f32[128,1024]{1,0:T(8,128)} fusion(f32[128,1024]{1,0:T(8,128)S(1)} %all_gather.16, f32[1024,1024]{1,0:T(8,128)} %param.7), kind=kOutput, calls=%fused_computation.64 | convolution fusion | flops 1610612736 | bytes 5242880 | tf_op jit(solution)/shard_map/dot_general | solution.py:73
  62.1 73.1 %all-reduce.6.cloned.1.call-done = f32[128,1024]{1,0:T(8,128)} async-done(((f32[128,1024]{1,0:T(8,128)}), f32[128,1024]{1,0:T(8,128)}) %all-reduce.6.cloned.1.call-update) | async-done | bytes 524304 | tf_op jit(solution)/shard_map/psum | solution.py:78
  135.2 7.4 %fusion = f32[128,1024]{1,0:T(8,128)} fusion(f32[1024,1024]{1,0:T(8,128)} %param.7, f32[128,1024]{1,0:T(8,128)} %all-reduce.6.cloned.1.call-done, f32[128,1024]{1,0:T(8,128)S(1)} %copy-done, f32[1024]{0:T(1024)S(1)} %broadcast_subtract_fusion, f32[1024]{0:T(1024)S(1)} %copy-done.7), kind=kOutput, calls=%fused_computation.9 | convolution fusion | flops 1611005952 | bytes 5775360 | tf_op jit(solution)/shard_map/ec,wc->ew/dot_general | solution.py:47
  143.0 20.7 %reduce-scatter.7.cloned.1.call-done = f32[32,1024]{1,0:T(8,128)} async-done(((f32[128,1024]{1,0:T(8,128)}), f32[32,1024]{1,0:T(8,128)}) %reduce-scatter.7.cloned.1.call-update) | async-done | bytes 131088 | tf_op jit(solution)/shard_map/reduce_scatter | solution.py:46
  164.7 6.8 %all_gather.17 = f32[128,1024]{1,0:T(8,128)S(1)} all-gather(f32[32,1024]{1,0:T(8,128)S(1)} %bitcast_add_fusion.2), channel_id=1, replica_groups=mesh['rows'=8,'cols'=4] {'cols'}, dimensions={0}, use_global_device_ids=true | all-gather | bytes 655360 | tf_op jit(solution)/shard_map/all_gather | solution.py:74
  171.5 5.4 %fusion.42 = f32[128,1024]{1,0:T(8,128)} fusion(f32[128,1024]{1,0:T(8,128)S(1)} %all_gather.17, f32[1024,1024]{1,0:T(8,128)} %param.7), kind=kOutput, calls=%fused_computation.65 | convolution fusion | flops 1610612736 | bytes 5242880 | tf_op jit(solution)/shard_map/dot_general | solution.py:73
  176.9 73.3 %all-reduce.8.cloned.1.call-done = f32[128,1024]{1,0:T(8,128)} async-done(((f32[128,1024]{1,0:T(8,128)}), f32[128,1024]{1,0:T(8,128)}) %all-reduce.8.cloned.1.call-update) | async-done | bytes 524304 | tf_op jit(solution)/shard_map/psum | solution.py:78
  250.3 1.2 multiply_add_fusion.2
  251.4 7.3 %fusion.43 = f32[128,1024]{1,0:T(8,128)} fusion(f32[128,1024]{1,0:T(8,128)S(1)} %multiply_add_fusion.2, f32[1024,1024]{1,0:T(8,128)} %param.7), kind=kOutput, calls=%fused_computation.66 | convolution fusion | flops 1610612736 | bytes 5242880 | tf_op jit(solution)/shard_map/ec,wc->ew/dot_general | solution.py:47
  259.1 20.7 %reduce-scatter.9.cloned.1.call-done = f32[32,1024]{1,0:T(8,128)} async-done(((f32[128,1024]{1,0:T(8,128)}), f32[32,1024]{1,0:T(8,128)}) %reduce-scatter.9.cloned.1.call-update) | async-done | bytes 131088 | tf_op jit(solution)/shard_map/reduce_scatter | solution.py:46
  280.9 6.6 %all_gather.18 = f32[128,1024]{1,0:T(8,128)S(1)} all-gather(f32[32,1024]{1,0:T(8,128)S(1)} %bitcast_add_fusion.1), channel_id=1, replica_groups=mesh['rows'=8,'cols'=4] {'cols'}, dimensions={0}, use_global_device_ids=true | all-gather | bytes 655360 | tf_op jit(solution)/shard_map/all_gather | solution.py:74
  287.5 5.4 %fusion.44 = f32[128,1024]{1,0:T(8,128)} fusion(f32[128,1024]{1,0:T(8,128)S(1)} %all_gather.18, f32[1024,1024]{1,0:T(8,128)} %param.7), kind=kOutput, calls=%fused_computation.67 | convolution fusion | flops 1610612736 | bytes 5242880 | tf_op jit(solution)/shard_map/dot_general | solution.py:73
  293.0 73.3 %all-reduce.10.cloned.1.call-done = f32[128,1024]{1,0:T(8,128)} async-done(((f32[128,1024]{1,0:T(8,128)}), f32[128,1024]{1,0:T(8,128)}) %all-reduce.10.cloned.1.call-update) | async-done | bytes 524304 | tf_op jit(solution)/shard_map/psum | solution.py:78
  366.3 7.4 %fusion.1 = f32[128,1024]{1,0:T(8,128)} fusion(f32[1024,1024]{1,0:T(8,128)} %param.7, f32[128,1024]{1,0:T(8,128)} %all-reduce.10.cloned.1.call-done, f32[128,1024]{1,0:T(8,128)S(1)} %multiply_add_fusion.2, f32[1024]{0:T(1024)S(1)} %broadcast_subtract_fusion, f32[1024]{0:T(1024)S(1)} %copy-done.7), kind=kOutput, calls=%fused_computation.10 | convolution fusion | flops 1611005952 | bytes 5775360 | tf_op jit(solution)/shard_map/ec,wc->ew/dot_general | solution.py:47
  376.0 18.7 %reduce-scatter.11.cloned.1.call-done = f32[32,1024]{1,0:T(8,128)} async-done(((f32[128,1024]{1,0:T(8,128)}), f32[32,1024]{1,0:T(8,128)}) %reduce-scatter.11.cloned.1.call-update) | async-done | bytes 131088 | tf_op jit(solution)/shard_map/reduce_scatter | solution.py:46
  394.8 1.0 bitcast_add_fusion
  395.8 6.6 %all_gather.19 = f32[128,1024]{1,0:T(8,128)S(1)} all-gather(f32[32,1024]{1,0:T(8,128)S(1)} %bitcast_add_fusion), channel_id=1, replica_groups=mesh['rows'=8,'cols'=4] {'cols'}, dimensions={0}, use_global_device_ids=true | all-gather | bytes 655360 | tf_op jit(solution)/shard_map/all_gather | solution.py:74
  402.4 5.4 %fusion.45 = f32[128,1024]{1,0:T(8,128)} fusion(f32[128,1024]{1,0:T(8,128)S(1)} %all_gather.19, f32[1024,1024]{1,0:T(8,128)} %param.7), kind=kOutput, calls=%fused_computation.68 | convolution fusion | flops 1610612736 | bytes 5242880 | tf_op jit(solution)/shard_map/dot_general | solution.py:73
  408.8 39.0 %all-reduce = f32[4,32,64]{1,0,2:T(4,128)S(1)} all-reduce(f32[4,32,64]{1,0,2:T(4,128)S(1)} %copy.30), channel_id=6, replica_groups=mesh['rows'=8,'cols'=4] {'rows'}, use_global_device_ids=true, to_apply=%region_13.14.clone | all-reduce | flops 8192 | bytes 65536
  448.5 33.4 %all-reduce.12.cloned.1.call-done = f32[128,1024]{1,0:T(8,128)} async-done(((f32[128,1024]{1,0:T(8,128)}), f32[128,1024]{1,0:T(8,128)}) %all-reduce.12.cloned.1.call-update) | async-done | bytes 524304 | tf_op jit(solution)/shard_map/psum | solution.py:78
  481.9 2.0 multiply_add_fusion
  (79 shorter events, 8.5 us)
Async XLA Ops:
  7.2 7.7 %copy-start.11 = (s32[8]{0:T(128)S(1)}, s32[8]{0:T(128)}, u32[]{:S(2)}) copy-start(s32[8]{0:T(128)} %param.11) | copy-start | bytes 100
  7.2 7.7 %copy-start.10 = (s32[64]{0:T(128)S(1)}, s32[64]{0:T(128)}, u32[]{:S(2)}) copy-start(s32[64]{0:T(128)} %param.12) | copy-start | bytes 772
  7.2 8.6 %copy-start.9 = (f32[4,128,8]{1,2,0:T(8,128)S(1)}, f32[4,128,8]{1,2,0:T(8,128)}, u32[]{:S(2)}) copy-start(f32[4,128,8]{1,2,0:T(8,128)} %param.13) | copy-start | bytes 49156
  7.2 41.3 %copy-start.8 = (f32[1024]{0:T(1024)S(1)}, f32[1024]{0:T(1024)}, u32[]{:S(2)}) copy-start(f32[1024]{0:T(1024)} %param.10) | copy-start | bytes 12292
  7.2 41.2 %reduce-scatter.5.cloned.1.call-start = ((), (), s32[]{:S(2)}) async-start(), calls=%async_computation.4 | async-start | bytes 655360 | tf_op jit(solution)/shard_map/reduce_scatter | solution.py:46
  14.8 47.3 %copy-start.7 = (f32[1024]{0:T(1024)S(1)}, f32[1024]{0:T(1024)}, u32[]{:S(2)}) copy-start(f32[1024]{0:T(1024)} %param.9) | copy-start | bytes 12292
  14.8 120.4 %copy-start = (f32[128,1024]{1,0:T(8,128)S(1)}, f32[128,1024]{1,0:T(8,128)}, u32[]{:S(2)}) copy-start(f32[128,1024]{1,0:T(8,128)} %param.8) | copy-start | bytes 1572868
  14.8 120.4 %all-reduce.6.cloned.1.call-start = ((), (), s32[]{:S(2)}) async-start(), calls=%async_computation.5 | async-start | bytes 1048576 | tf_op jit(solution)/shard_map/psum | solution.py:78
  62.0 101.6 %reduce-scatter.7.cloned.1.call-start = ((), (), s32[]{:S(2)}) async-start(), calls=%async_computation.6 | async-start | bytes 655360 | tf_op jit(solution)/shard_map/reduce_scatter | solution.py:46
  142.6 107.7 %copy-start.2 = (f32[128,1024]{1,0:T(8,128)S(1)}, f32[128,1024]{1,0:T(8,128)}, u32[]{:S(2)}) copy-start(f32[128,1024]{1,0:T(8,128)} %all-reduce.6.cloned.1.call-done) | copy-start | bytes 1572868
  142.6 107.6 %all-reduce.8.cloned.1.call-start = ((), (), s32[]{:S(2)}) async-start(), calls=%async_computation.7 | async-start | bytes 1048576 | tf_op jit(solution)/shard_map/psum | solution.py:78
  176.9 103.0 %reduce-scatter.9.cloned.1.call-start = ((), (), s32[]{:S(2)}) async-start(), calls=%async_computation.8 | async-start | bytes 655360 | tf_op jit(solution)/shard_map/reduce_scatter | solution.py:46
  258.8 107.5 %all-reduce.10.cloned.1.call-start = ((), (), s32[]{:S(2)}) async-start(), calls=%async_computation.9 | async-start | bytes 1048576 | tf_op jit(solution)/shard_map/psum | solution.py:78
  292.9 81.1 %copy-start.12 = (u32[32]{0:T(128)S(1)}, u32[32]{0:T(128)}, u32[]{:S(2)}) copy-start(u32[32]{0:T(128)} %constant.42) | copy-start | bytes 388
  292.9 82.6 %copy-start.3 = (f32[32,1024]{1,0:T(8,128)S(1)}, f32[32,1024]{1,0:T(8,128)}, u32[]{:S(2)}) copy-start(f32[32,1024]{1,0:T(8,128)} %reduce-scatter.5.cloned.1.call-done) | copy-start | bytes 393220
  292.9 83.0 %copy-start.4 = (f32[32,1024]{1,0:T(8,128)S(1)}, f32[32,1024]{1,0:T(8,128)}, u32[]{:S(2)}) copy-start(f32[32,1024]{1,0:T(8,128)} %reduce-scatter.7.cloned.1.call-done) | copy-start | bytes 393220
  292.9 101.8 %reduce-scatter.11.cloned.1.call-start = ((), (), s32[]{:S(2)}) async-start(), calls=%async_computation.10 | async-start | bytes 655360 | tf_op jit(solution)/shard_map/reduce_scatter | solution.py:46
  373.7 34.3 %copy-start.6 = (f32[32,1024]{1,0:T(8,128)S(1)}, f32[32,1024]{1,0:T(8,128)}, u32[]{:S(2)}) copy-start(f32[32,1024]{1,0:T(8,128)} %reduce-scatter.9.cloned.1.call-done) | copy-start | bytes 393220
  373.7 108.2 %all-reduce.12.cloned.1.call-start = ((), (), s32[]{:S(2)}) async-start(), calls=%async_computation.11 | async-start | bytes 1048576 | tf_op jit(solution)/shard_map/psum | solution.py:78
  394.7 13.7 %copy-start.5 = (f32[32,1024]{1,0:T(8,128)S(1)}, f32[32,1024]{1,0:T(8,128)}, u32[]{:S(2)}) copy-start(f32[32,1024]{1,0:T(8,128)} %reduce-scatter.11.cloned.1.call-done) | copy-start | bytes 393220
  394.8 87.1 %copy-start.1 = (f32[128,1024]{1,0:T(8,128)S(1)}, f32[128,1024]{1,0:T(8,128)}, u32[]{:S(2)}) copy-start(f32[128,1024]{1,0:T(8,128)} %all-reduce.10.cloned.1.call-done) | copy-start | bytes 1572868
Sparse Core Ops, SparseCore 0:
  14.9 24.3 reduce-scatter.4
  62.2 72.9 all-reduce.5
  142.7 20.8 reduce-scatter.6
  177.0 73.2 all-reduce.7
  258.9 20.8 reduce-scatter.8
  293.0 73.1 all-reduce.9
  373.8 20.8 reduce-scatter.10
  407.9 73.9 all-reduce.11
where the time goes:
time: 491 us
  waiting for transfers between devices  313 us (64%)
  blocking collectives  98.5 us (20%)
  matrix products  53.1 us (11%)
  between operations  15.1 us (3%)
  other arithmetic  7.63 us (2%)
    psum x4, waiting for transfers between devices, shards(): driven = lax.psum(driven_part, 'rows')  253 us
    reduce_scatter x4, waiting for transfers between devices, shards(): lax.psum_scatter(jnp.einsum('ec,wc->ew', current, projector_matrix, preci...  60.1 us
    unnamed x1, blocking collectives  39 us
    all_gather x1, blocking collectives, shards(): all_power = lax.all_gather(owner_power, 'rows', axis=2, tiled=True)  32.3 us
    dot_general x4, matrix products, shards(): jnp.einsum('ec,wc->ew', current, projector_matrix, precision=dominant_spe...  29.7 us
    all_gather x4, blocking collectives, shards(): lax.all_gather(heating_at_points, 'cols', axis=0, tiled=True)  27.2 us
    dot_general x4, matrix products, shards(): jnp.dot(lax.all_gather(heating_at_points, 'cols', axis=0, tiled=True), pr...  21.5 us
  transfers between devices with their start and end apart: 8, of which 7 were waited for; matrix products, arithmetic and copies ran while one was open for 1% of the time, Pallas kernels for 0%

commit v1 on v0

v1 whole, which is shorter than its diff:
```python
import functools

import jax
import jax.numpy as jnp
from jax import lax
from jax.experimental import pallas as pl
from jax.experimental.pallas import tpu as pltpu
from jax.sharding import PartitionSpec as P

STEPS = 4
PATCH_POINTS = 128
GROUPS = 2
LAG = 4
BLOCK = 256
MESH = pl.DeviceIdType.MESH
ORDERS = ((0, 1, 2), (1, 0, 2))


def log2(n):
    return n.bit_length() - 1


def split(x):
    hi = x.astype(jnp.bfloat16)
    return hi, (x - hi.astype(jnp.float32)).astype(jnp.bfloat16)


def dot(a, b, dims):
    return lax.dot_general(a, b, (dims, ((), ())), preferred_element_type=jnp.float32)


NN = ((1,), (0,))
NT = ((1,), (1,))


def kernel(
    n_rows, n_cols, p_ref, start_ref, decay_ref, escape_ref, nodepos_ref, power_ref,
    final_ref, temps_ref, hist_ref,
    p_hi, p_lo, spread, state, lhs, t_part, t_rx, t_full, d_part, d_rx, d_full,
    all_power, power_t, shares, h_part, h_rx, send_sem, recv_sem,
):
    r, q = lax.axis_index("rows"), lax.axis_index("cols")
    kr, kc = log2(n_rows), log2(n_cols)
    scen, states = start_ref.shape
    nodes = p_ref.shape[0]
    size = scen // GROUPS
    tiles = size // 8
    share = scen // n_cols
    positions = spread.shape[0]

    def bit(i, b):
        return (i // (1 << b)) % 2

    def flip(i, b):
        return i + (1 - 2 * bit(i, b)) * (1 << b)

    def row_peer(b):
        return (flip(r, b), q)

    def col_peer(b):
        return (r, flip(q, b))

    barrier = pltpu.get_barrier_semaphore()
    peers = [row_peer(b) for b in range(kr)] + [col_peer(b) for b in range(kc)]
    for peer in peers:
        pl.semaphore_signal(barrier, inc=1, device_id=peer, device_id_type=MESH)

    state[...] = start_ref[...]
    used = [0]
    copies = []

    def send(src, dst, peer):
        slot = used[0]
        used[0] += 1
        copy = pltpu.make_async_remote_copy(
            src_ref=src, dst_ref=dst, send_sem=send_sem.at[slot], recv_sem=recv_sem.at[slot],
            device_id=peer, device_id_type=MESH,
        )
        copy.start()
        copies.append(copy)
        return copy

    @pl.loop(0, nodes // BLOCK)
    def _(i):
        at = pl.ds(pl.multiple_of(i * BLOCK, BLOCK), BLOCK)
        hi, lo = split(p_ref[at, :])
        p_hi[at, :] = hi
        p_lo[at, :] = lo

    rows_iota = lax.broadcasted_iota(jnp.int32, (positions, nodes), 0)
    spread[...] = jnp.where(rows_iota == nodepos_ref[...], 1.0, 0.0).astype(jnp.bfloat16)
    pl.semaphore_wait(barrier, len(peers))

    ready = []

    def power_chain():
        all_power[pl.ds(r, 1)] = power_ref[...][None]
        for b in range(kr):
            block = pl.ds((r // (1 << b)) * (1 << b), 1 << b)
            copy = send(all_power.at[block], all_power.at[block], row_peer(b))
            yield
            copy.wait_recv()
        for k in range(STEPS):
            table = all_power[:, k].reshape(positions, scen).T
            hi, lo = split(table)
            power_t[k, 0] = hi
            power_t[k, 1] = lo
        ready.append(True)

    def history_chain():
        hi, lo = split(shares[...].reshape(STEPS * share, nodes))
        both = dot(spread[...], hi, NT) + dot(spread[...], lo, NT)
        h_part[...] = (both * (1.0 / PATCH_POINTS)).reshape(n_rows, 8, STEPS * share)
        start, length, at = 0, n_rows, 0
        for b in reversed(range(kr)):
            length //= 2
            keep = start + bit(r, b) * length
            away = start + (1 - bit(r, b)) * length
            copy = send(h_part.at[pl.ds(away, length)], h_rx.at[pl.ds(at, length)], row_peer(b))
            yield
            copy.wait_recv()
            kept = pl.ds(keep, length)
            h_part[kept] = h_part[kept] + h_rx[pl.ds(at, length)]
            start, at = keep, at + length
        hist_ref[...] = h_part[pl.ds(r, 1)][0]

    extra = []

    def chain(g):
        mine = slice(g * size, (g + 1) * size)
        width = d_part.shape[-1]
        units = d_part.shape[1] // GROUPS
        unit0 = g * units
        order = ORDERS[g % 2] if kr == 3 else tuple(range(kr))

        def load_lhs():
            for c in range(0, states, BLOCK):
                hi, lo = split(state[mine, c : c + BLOCK])
                lhs[g, :size, c : c + BLOCK] = hi
                lhs[g, size:, c : c + BLOCK] = lo

        load_lhs()
        for k in range(STEPS):

            @pl.loop(0, nodes // BLOCK)
            def _(i):
                at = pl.ds(pl.multiple_of(i * BLOCK, BLOCK), BLOCK)
                two = dot(lhs[g], p_hi[at, :], NT)
                out = two[:size] + two[size:] + dot(lhs[g, :size], p_lo[at, :], NT)
                t_part[k, pl.ds(g * tiles, tiles), :, at] = out.reshape(tiles, 8, BLOCK)

            start, length, at = g * tiles, tiles, g * tiles
            for b in range(kc - 1):
                length //= 2
                keep = start + bit(q, b) * length
                away = start + (1 - bit(q, b)) * length
                copy = send(t_part.at[k, pl.ds(away, length)], t_rx.at[k, pl.ds(at, length)], col_peer(b))
                yield
                copy.wait_recv()
                kept = pl.ds(keep, length)
                t_part[k, kept] = t_part[k, kept] + t_rx[k, pl.ds(at, length)]
                start, at = keep, at + length
            kept = pl.ds(start, length)
            copy = send(t_part.at[k, kept], t_rx.at[k, pl.ds(at, length)], col_peer(kc - 1))
            yield
            copy.wait_recv()
            t_full[k, kept] = t_part[k, kept] + t_rx[k, pl.ds(at, length)]
            for b in reversed(range(kc - 1)):
                kept = pl.ds(start, length)
                copy = send(t_full.at[k, kept], t_full.at[k, kept], col_peer(b))
                yield
                copy.wait_recv()
                start, length = start - bit(q, b) * length, 2 * length

            if g == GROUPS - 1:
                own = t_full[k, pl.ds(q * (share // 8), share // 8)]
                shares[k] = own.reshape(share, nodes)
                if k == STEPS - 1:
                    temps_ref[...] = own.reshape(share, nodes)
                    extra.append(history_chain())

            while not ready:
                yield

            @pl.loop(0, nodes // BLOCK)
            def _(i):
                at = pl.ds(pl.multiple_of(i * BLOCK, BLOCK), BLOCK)
                heat = dot(power_t[k, 0, mine], spread[:, at], NN) + dot(power_t[k, 1, mine], spread[:, at], NN)
                temp = t_full[k, pl.ds(g * tiles, tiles), :, at].reshape(size, BLOCK)
                hi, lo = split(heat + escape_ref[:, at] * (1.0 + jnp.tanh(2.0 * temp)))
                lhs[g, :size, at] = hi
                lhs[g, size:, at] = lo

            @pl.loop(0, states // BLOCK)
            def _(i):
                at = pl.ds(pl.multiple_of(i * BLOCK, BLOCK), BLOCK)
                two = dot(lhs[g], p_hi[:, at], NN)
                out = two[:size] + two[size:] + dot(lhs[g, :size], p_lo[:, at], NN)
                unit = (i * BLOCK) // width
                inner = pl.ds(pl.multiple_of((i * BLOCK) % width, BLOCK), BLOCK)
                d_part[k, pl.ds(unit0 + unit * tiles, tiles), :, inner] = out.reshape(tiles, 8, BLOCK)

            start, length, at = unit0, units, unit0
            for b in order[:-1]:
                length //= 2
                keep = start + bit(r, b) * length
                away = start + (1 - bit(r, b)) * length
                copy = send(d_part.at[k, pl.ds(away, length)], d_rx.at[k, pl.ds(at, length)], row_peer(b))
                yield
                copy.wait_recv()
                kept = pl.ds(keep, length)
                d_part[k, kept] = d_part[k, kept] + d_rx[k, pl.ds(at, length)]
                start, at = keep, at + length
            kept = pl.ds(start, length)
            copy = send(d_part.at[k, kept], d_rx.at[k, pl.ds(at, length)], row_peer(order[-1]))
            yield
            copy.wait_recv()
            d_full[k, kept] = d_part[k, kept] + d_rx[k, pl.ds(at, length)]
            for b in reversed(order[:-1]):
                kept = pl.ds(start, length)
                copy = send(d_full.at[k, kept], d_full.at[k, kept], row_peer(b))
                yield
                copy.wait_recv()
                start, length = start - bit(r, b) * length, 2 * length

            for j in range(states // width):
                cols = slice(j * width, (j + 1) * width)
                keep_share = decay_ref[:, cols]
                driven = d_full[k, unit0 + j * tiles : unit0 + (j + 1) * tiles].reshape(size, width)
                state[mine, cols] = keep_share * state[mine, cols] + (1.0 - keep_share) * driven
            if k < STEPS - 1:
                load_lhs()
            else:
                final_ref[mine, :] = state[mine, :]

    running = [(0, power_chain())] + [(g * LAG, chain(g)) for g in range(GROUPS)]
    tick = 0
    while running or extra:
        running += [(tick, c) for c in extra]
        extra.clear()
        left = []
        for when, c in running:
            if when > tick:
                left.append((when, c))
                continue
            try:
                next(c)
                left.append((when, c))
            except StopIteration:
                pass
        running = left
        tick += 1
    for copy in copies:
        copy.wait_send()


def shards(projector_matrix, start_state, decay_rate, escape_heat_factor, tile_block, block_owner, owner_power):
    n_rows, n_cols = lax.axis_size("rows"), lax.axis_size("cols")
    kr, kc = log2(n_rows), log2(n_cols)
    nodes, states = projector_matrix.shape
    scen = start_state.shape[0]
    share = scen // n_cols
    per_owner = owner_power.shape[2]
    blocks = block_owner.shape[0]
    ids = jnp.arange(blocks, dtype=jnp.int32)
    same = (block_owner[:, None] == block_owner[None, :]) & (ids[None, :] < ids[:, None])
    position = block_owner * per_owner + jnp.sum(same.astype(jnp.int32), axis=1)
    tile_position = jnp.sum(jnp.where(tile_block[:, None] == ids[None, :], position[None, :], 0), axis=1)
    node_position = jnp.repeat(tile_position, PATCH_POINTS)[None, :]
    size = scen // GROUPS
    tiles = size // 8
    need = n_rows // 2
    width = states
    while (tiles * (states // width)) % need:
        width //= 2
    units = GROUPS * tiles * (states // width)
    sems = STEPS * GROUPS * (2 * kr - 1 + 2 * kc - 1) + 2 * kr
    f32, b16 = jnp.float32, jnp.bfloat16
    vmem = pl.BlockSpec(memory_space=pltpu.VMEM)
    final, temps, hist = pl.pallas_call(
        functools.partial(kernel, n_rows, n_cols),
        out_shape=(
            jax.ShapeDtypeStruct((scen, states), f32),
            jax.ShapeDtypeStruct((share, nodes), f32),
            jax.ShapeDtypeStruct((per_owner, STEPS * share), f32),
        ),
        in_specs=[vmem] * 6,
        out_specs=(vmem,) * 3,
        scratch_shapes=[
            pltpu.VMEM((nodes, states), b16),
            pltpu.VMEM((nodes, states), b16),
            pltpu.VMEM((blocks, nodes), b16),
            pltpu.VMEM((scen, states), f32),
            pltpu.VMEM((GROUPS, 2 * size, max(states, nodes)), b16),
            pltpu.VMEM((STEPS, scen // 8, 8, nodes), f32),
            pltpu.VMEM((STEPS, scen // 8, 8, nodes), f32),
            pltpu.VMEM((STEPS, scen // 8, 8, nodes), f32),
            pltpu.VMEM((STEPS, units, 8, width), f32),
            pltpu.VMEM((STEPS, units, 8, width), f32),
            pltpu.VMEM((STEPS, units, 8, width), f32),
            pltpu.VMEM((n_rows, STEPS, per_owner, scen), f32),
            pltpu.VMEM((STEPS, 2, scen, blocks), b16),
            pltpu.VMEM((STEPS, share, nodes), f32),
            pltpu.VMEM((n_rows, per_owner, STEPS * share), f32),
            pltpu.VMEM((n_rows, per_owner, STEPS * share), f32),
            pltpu.SemaphoreType.DMA((sems,)),
            pltpu.SemaphoreType.DMA((sems,)),
        ],
        compiler_params=pltpu.CompilerParams(
            collective_id=0, has_side_effects=True, vmem_limit_bytes=60 * 1024 * 1024
        ),
    )(
        projector_matrix, start_state, decay_rate[None, :], escape_heat_factor[None, :],
        node_position, jnp.transpose(owner_power, (0, 2, 1)),
    )
    history = jnp.transpose(hist.reshape(per_owner, STEPS, share), (1, 2, 0))
    return final, temps, history


def solution(mesh):
    placed = (
        P("rows", "cols"),
        P(None, "cols"),
        P("cols"),
        P("rows"),
        P("rows"),
        P(),
        P(None, None, "rows"),
    )
    return jax.shard_map(
        shards,
        mesh=mesh,
        in_specs=placed,
        out_specs=(P(None, "cols"), P("cols", "rows"), P(None, "cols", "rows")),
        check_vma=False,
    )
```

time: 491 us -> 157 us (0.32)
  waiting for transfers between devices: 313 us -> 0 us
  Pallas kernels: 0 us -> 148 us
  blocking collectives: 98.5 us -> 0 us
  matrix products: 53.1 us -> 0 us
  between operations: 15.1 us -> 0.64 us
  other arithmetic: 7.63 us -> 2.41 us
    psum x4 -> x0, waiting for transfers between devices: 253 us -> none  [shards(): driven = lax.psum(driven_part, 'rows')]
    pallas_call x0 -> x1, Pallas kernels: none -> 148 us  [shards(): pl.pallas_call(functools.partial(kernel, n_rows, n_cols), out_shape=(jax....]
    reduce_scatter x4 -> x0, waiting for transfers between devices: 60.1 us -> none  [shards(): lax.psum_scatter(jnp.einsum('ec,wc->ew', current, projector_matrix, preci...]
    all_gather x5 -> x0, blocking collectives: 59.5 us -> none  [the longest x1 32.3 us: shards(): all_power = lax.all_gather(owner_power, 'rows', axis=2, tiled=True)]
    dot_general x16 -> x0, matrix products: 53.1 us -> none  [the longest x4 29.7 us: shards(): jnp.einsum('ec,wc->ew', current, projector_matrix, precision=dominant_spe...]
    unnamed x1 -> x0, blocking collectives: 39 us -> none
    add x7 -> x1, other arithmetic: 7 us -> 0.67 us  [shards(): position = block_owner * per_owner + jnp.sum(same.astype(jnp.int32), axis=1)]
  transfers between devices with their start and end apart: 8 -> 0, of which waited for: 7 -> 0; matrix products, arithmetic and copies ran while one was open for 1% -> 0% of each run, Pallas kernels for 0% -> 0%
where the time goes in v1:
time: 157 us
  Pallas kernels  148 us (94%)
  local copies, waits for them, and re-layouts  5.47 us (3%)
  other arithmetic  2.41 us (2%)
    pallas_call x1, Pallas kernels, shards(): pl.pallas_call(functools.partial(kernel, n_rows, n_cols), out_shape=(jax....  148 us
    unnamed x2, local copies, waits for them, and re-layouts  3.45 us

profile of v1, /device:TPU:0, one launch (start us, length us, event | category | flops | bytes accessed | tf_op | source)
XLA Modules:
  0.0 156.8 jit_solution(16225836367764648417)
XLA Ops:
  0.6 0.9 convert_reduce_fusion
  1.5 0.7 multiply_add_fusion
  2.2 0.8 select_reduce_fusion
  3.0 0.7 broadcast_in_dim.32
  3.7 148.3 %shard_map.94 = (f32[128,1024]{1,0:T(8,128)}, f32[32,1024]{1,0:T(8,128)}, f32[8,128]{1,0:T(8,128)}) custom-call(f32[1024,1024]{1,0:T(8,128)} %p_ref.1, f32[128,1024]{1,0:T(8,128)} %start_ref.1, f32[1,1024]{1,0:T(1,128)} %bitcast.10, f32[1,1024]{1,0:T(1,128)} %bitcast.11, s32[1,1024]{1,0:T(1,128)} %bitcast.9, f32[4,8,128]{2,1,0:T(8,128)} %bitcast.7), custom_call_target="tpu_custom_call" | custom-call | tf_op jit(solution)/shard_map/pallas_call | solution.py:280
  152.0 0.7 reshape.13
  152.8 0.6 copy.13
  153.4 1.9 %copy.16 = f32[128,1024]{1,0:T(8,128)} copy(f32[128,1024]{1,0:T(8,128)} %get-tuple-element.12) | data formatting | bytes 1048576
  155.3 1.6 copy.17

commit v2 on v1

--- a/solution.py
+++ b/solution.py
@@ -9,8 +9,9 @@
 
 STEPS = 4
 PATCH_POINTS = 128
-GROUPS = 2
-LAG = 4
+GROUPS = 1
+LAG = 0
+CHUNKS = 4
 BLOCK = 256
 MESH = pl.DeviceIdType.MESH
 ORDERS = ((0, 1, 2), (1, 0, 2))
@@ -126,12 +127,67 @@
 
     extra = []
 
+    def together(parts):
+        while parts:
+            parts = [part for part in parts if next(part, parts) is not parts]
+            if parts:
+                yield
+
+    def cols_chain(k, g, c):
+        start, length, at = g * tiles, tiles, g * tiles
+        for b in range(kc - 1):
+            length //= 2
+            keep = start + bit(q, b) * length
+            away = start + (1 - bit(q, b)) * length
+            copy = send(t_part.at[k, c, pl.ds(away, length)], t_rx.at[k, c, pl.ds(at, length)], col_peer(b))
+            yield
+            copy.wait_recv()
+            kept = pl.ds(keep, length)
+            t_part[k, c, kept] = t_part[k, c, kept] + t_rx[k, c, pl.ds(at, length)]
+            start, at = keep, at + length
+        kept = pl.ds(start, length)
+        copy = send(t_part.at[k, c, kept], t_rx.at[k, c, pl.ds(at, length)], col_peer(kc - 1))
+        yield
+        copy.wait_recv()
+        t_full[k, c, kept] = t_part[k, c, kept] + t_rx[k, c, pl.ds(at, length)]
+        for b in reversed(range(kc - 1)):
+            kept = pl.ds(start, length)
+            copy = send(t_full.at[k, c, kept], t_full.at[k, c, kept], col_peer(b))
+            yield
+            copy.wait_recv()
+            start, length = start - bit(q, b) * length, 2 * length
+
+    def rows_chain(k, g, c):
+        units = d_part.shape[2] // GROUPS
+        order = ORDERS[(g + c) % 2] if kr == 3 else tuple(range(kr))
+        start, length, at = g * units, units, g * units
+        for b in order[:-1]:
+            length //= 2
+            keep = start + bit(r, b) * length
+            away = start + (1 - bit(r, b)) * length
+            copy = send(d_part.at[k, c, pl.ds(away, length)], d_rx.at[k, c, pl.ds(at, length)], row_peer(b))
+            yield
+            copy.wait_recv()
+            kept = pl.ds(keep, length)
+            d_part[k, c, kept] = d_part[k, c, kept] + d_rx[k, c, pl.ds(at, length)]
+            start, at = keep, at + length
+        kept = pl.ds(start, length)
+        copy = send(d_part.at[k, c, kept], d_rx.at[k, c, pl.ds(at, length)], row_peer(order[-1]))
+        yield
+        copy.wait_recv()
+        d_full[k, c, kept] = d_part[k, c, kept] + d_rx[k, c, pl.ds(at, length)]
+        for b in reversed(order[:-1]):
+            kept = pl.ds(start, length)
+            copy = send(d_full.at[k, c, kept], d_full.at[k, c, kept], row_peer(b))
+            yield
+            copy.wait_recv()
+            start, length = start - bit(r, b) * length, 2 * length
+
     def chain(g):
         mine = slice(g * size, (g + 1) * size)
         width = d_part.shape[-1]
-        units = d_part.shape[1] // GROUPS
-        unit0 = g * units
-        order = ORDERS[g % 2] if kr == 3 else tuple(range(kr))
+        unit0 = g * (d_part.shape[2] // GROUPS)
+        piece, strip = nodes // CHUNKS, states // CHUNKS
 
         def load_lhs():
             for c in range(0, states, BLOCK):
@@ -141,93 +197,69 @@
 
         load_lhs()
         for k in range(STEPS):
-
-            @pl.loop(0, nodes // BLOCK)
-            def _(i):
-                at = pl.ds(pl.multiple_of(i * BLOCK, BLOCK), BLOCK)
-                two = dot(lhs[g], p_hi[at, :], NT)
-                out = two[:size] + two[size:] + dot(lhs[g, :size], p_lo[at, :], NT)
-                t_part[k, pl.ds(g * tiles, tiles), :, at] = out.reshape(tiles, 8, BLOCK)
-
-            start, length, at = g * tiles, tiles, g * tiles
-            for b in range(kc - 1):
-                length //= 2
-                keep = start + bit(q, b) * length
-                away = start + (1 - bit(q, b)) * length
-                copy = send(t_part.at[k, pl.ds(away, length)], t_rx.at[k, pl.ds(at, length)], col_peer(b))
-                yield
-                copy.wait_recv()
-                kept = pl.ds(keep, length)
-                t_part[k, kept] = t_part[k, kept] + t_rx[k, pl.ds(at, length)]
-                start, at = keep, at + length
-            kept = pl.ds(start, length)
-            copy = send(t_part.at[k, kept], t_rx.at[k, pl.ds(at, length)], col_peer(kc - 1))
-            yield
-            copy.wait_recv()
-            t_full[k, kept] = t_part[k, kept] + t_rx[k, pl.ds(at, length)]
-            for b in reversed(range(kc - 1)):
-                kept = pl.ds(start, length)
-                copy = send(t_full.at[k, kept], t_full.at[k, kept], col_peer(b))
-                yield
-                copy.wait_recv()
-                start, length = start - bit(q, b) * length, 2 * length
+            parts = []
+            for c in range(CHUNKS):
+
+                @pl.loop(0, piece // BLOCK)
+                def _(i):
+                    local = pl.ds(pl.multiple_of(i * BLOCK, BLOCK), BLOCK)
+                    at = pl.ds(pl.multiple_of(c * piece + i * BLOCK, BLOCK), BLOCK)
+                    two = dot(lhs[g], p_hi[at, :], NT)
+                    out = two[:size] + two[size:] + dot(lhs[g, :size], p_lo[at, :], NT)
+                    t_part[k, c, pl.ds(g * tiles, tiles), :, local] = out.reshape(tiles, 8, BLOCK)
+
+                parts.append(cols_chain(k, g, c))
+                next(parts[-1])
+            yield
+            yield from together(parts)
 
             if g == GROUPS - 1:
-                own = t_full[k, pl.ds(q * (share // 8), share // 8)]
-                shares[k] = own.reshape(share, nodes)
+                for c in range(CHUNKS):
+                    own = t_full[k, c, pl.ds(q * (share // 8), share // 8)].reshape(share, piece)
+                    shares[k, :, c * piece : (c + 1) * piece] = own
+                    if k == STEPS - 1:
+                        temps_ref[:, c * piece : (c + 1) * piece] = own
                 if k == STEPS - 1:
-                    temps_ref[...] = own.reshape(share, nodes)
                     extra.append(history_chain())
 
             while not ready:
                 yield
 
-            @pl.loop(0, nodes // BLOCK)
-            def _(i):
-                at = pl.ds(pl.multiple_of(i * BLOCK, BLOCK), BLOCK)
-                heat = dot(power_t[k, 0, mine], spread[:, at], NN) + dot(power_t[k, 1, mine], spread[:, at], NN)
-                temp = t_full[k, pl.ds(g * tiles, tiles), :, at].reshape(size, BLOCK)
-                hi, lo = split(heat + escape_ref[:, at] * (1.0 + jnp.tanh(2.0 * temp)))
-                lhs[g, :size, at] = hi
-                lhs[g, size:, at] = lo
-
-            @pl.loop(0, states // BLOCK)
-            def _(i):
-                at = pl.ds(pl.multiple_of(i * BLOCK, BLOCK), BLOCK)
-                two = dot(lhs[g], p_hi[:, at], NN)
-                out = two[:size] + two[size:] + dot(lhs[g, :size], p_lo[:, at], NN)
-                unit = (i * BLOCK) // width
-                inner = pl.ds(pl.multiple_of((i * BLOCK) % width, BLOCK), BLOCK)
-                d_part[k, pl.ds(unit0 + unit * tiles, tiles), :, inner] = out.reshape(tiles, 8, BLOCK)
-
-            start, length, at = unit0, units, unit0
-            for b in order[:-1]:
-                length //= 2
-                keep = start + bit(r, b) * length
-                away = start + (1 - bit(r, b)) * length
-                copy = send(d_part.at[k, pl.ds(away, length)], d_rx.at[k, pl.ds(at, length)], row_peer(b))
-                yield
-                copy.wait_recv()
-                kept = pl.ds(keep, length)
-                d_part[k, kept] = d_part[k, kept] + d_rx[k, pl.ds(at, length)]
-                start, at = keep, at + length
-            kept = pl.ds(start, length)
-            copy = send(d_part.at[k, kept], d_rx.at[k, pl.ds(at, length)], row_peer(order[-1]))
-            yield
-            copy.wait_recv()
-            d_full[k, kept] = d_part[k, kept] + d_rx[k, pl.ds(at, length)]
-            for b in reversed(order[:-1]):
-                kept = pl.ds(start, length)
-                copy = send(d_full.at[k, kept], d_full.at[k, kept], row_peer(b))
-                yield
-                copy.wait_recv()
-                start, length = start - bit(r, b) * length, 2 * length
-
-            for j in range(states // width):
-                cols = slice(j * width, (j + 1) * width)
-                keep_share = decay_ref[:, cols]
-                driven = d_full[k, unit0 + j * tiles : unit0 + (j + 1) * tiles].reshape(size, width)
-                state[mine, cols] = keep_share * state[mine, cols] + (1.0 - keep_share) * driven
+            for c in range(CHUNKS):
+
+                @pl.loop(0, piece // BLOCK)
+                def _(i):
+                    local = pl.ds(pl.multiple_of(i * BLOCK, BLOCK), BLOCK)
+                    at = pl.ds(pl.multiple_of(c * piece + i * BLOCK, BLOCK), BLOCK)
+                    heat = dot(power_t[k, 0, mine], spread[:, at], NN) + dot(power_t[k, 1, mine], spread[:, at], NN)
+                    temp = t_full[k, c, pl.ds(g * tiles, tiles), :, local].reshape(size, BLOCK)
+                    hi, lo = split(heat + escape_ref[:, at] * (1.0 + jnp.tanh(2.0 * temp)))
+                    lhs[g, :size, at] = hi
+                    lhs[g, size:, at] = lo
+
+            parts = []
+            for c in range(CHUNKS):
+
+                @pl.loop(0, strip // BLOCK)
+                def _(i):
+                    at = pl.ds(pl.multiple_of(c * strip + i * BLOCK, BLOCK), BLOCK)
+                    two = dot(lhs[g], p_hi[:, at], NN)
+                    out = two[:size] + two[size:] + dot(lhs[g, :size], p_lo[:, at], NN)
+                    unit = (i * BLOCK) // width
+                    inner = pl.ds(pl.multiple_of((i * BLOCK) % width, BLOCK), BLOCK)
+                    d_part[k, c, pl.ds(unit0 + unit * tiles, tiles), :, inner] = out.reshape(tiles, 8, BLOCK)
+
+                parts.append(rows_chain(k, g, c))
+                next(parts[-1])
+            yield
+            yield from together(parts)
+
+            for c in range(CHUNKS):
+                for j in range(strip // width):
+                    cols = slice(c * strip + j * width, c * strip + (j + 1) * width)
+                    keep_share = decay_ref[:, cols]
+                    driven = d_full[k, c, unit0 + j * tiles : unit0 + (j + 1) * tiles].reshape(size, width)
+                    state[mine, cols] = keep_share * state[mine, cols] + (1.0 - keep_share) * driven
             if k < STEPS - 1:
                 load_lhs()
             else:
@@ -270,11 +302,11 @@
     size = scen // GROUPS
     tiles = size // 8
     need = n_rows // 2
-    width = states
-    while (tiles * (states // width)) % need:
+    width = states // CHUNKS
+    while (tiles * (states // CHUNKS // width)) % need:
         width //= 2
-    units = GROUPS * tiles * (states // width)
-    sems = STEPS * GROUPS * (2 * kr - 1 + 2 * kc - 1) + 2 * kr
+    units = GROUPS * tiles * (states // CHUNKS // width)
+    sems = STEPS * GROUPS * CHUNKS * (2 * kr - 1 + 2 * kc - 1) + 2 * kr
     f32, b16 = jnp.float32, jnp.bfloat16
     vmem = pl.BlockSpec(memory_space=pltpu.VMEM)
     final, temps, hist = pl.pallas_call(
@@ -292,12 +324,12 @@
             pltpu.VMEM((blocks, nodes), b16),
             pltpu.VMEM((scen, states), f32),
             pltpu.VMEM((GROUPS, 2 * size, max(states, nodes)), b16),
-            pltpu.VMEM((STEPS, scen // 8, 8, nodes), f32),
-            pltpu.VMEM((STEPS, scen // 8, 8, nodes), f32),
-            pltpu.VMEM((STEPS, scen // 8, 8, nodes), f32),
-            pltpu.VMEM((STEPS, units, 8, width), f32),
-            pltpu.VMEM((STEPS, units, 8, width), f32),
-            pltpu.VMEM((STEPS, units, 8, width), f32),
+            pltpu.VMEM((STEPS, CHUNKS, scen // 8, 8, nodes // CHUNKS), f32),
+            pltpu.VMEM((STEPS, CHUNKS, scen // 8, 8, nodes // CHUNKS), f32),
+            pltpu.VMEM((STEPS, CHUNKS, scen // 8, 8, nodes // CHUNKS), f32),
+            pltpu.VMEM((STEPS, CHUNKS, units, 8, width), f32),
+            pltpu.VMEM((STEPS, CHUNKS, units, 8, width), f32),
+            pltpu.VMEM((STEPS, CHUNKS, units, 8, width), f32),
             pltpu.VMEM((n_rows, STEPS, per_owner, scen), f32),
             pltpu.VMEM((STEPS, 2, scen, blocks), b16),
             pltpu.VMEM((STEPS, share, nodes), f32),

time: 157 us -> 144 us (0.917)
  Pallas kernels: 148 us -> 135 us
    pallas_call x1, Pallas kernels: 148 us -> 135 us  [shards(): pl.pallas_call(functools.partial(kernel, n_rows, n_cols), out_shape=(jax....]
where the time goes in v2:
time: 144 us
  Pallas kernels  135 us (94%)
  local copies, waits for them, and re-layouts  5.47 us (4%)
  other arithmetic  2.41 us (2%)
    pallas_call x1, Pallas kernels, shards(): pl.pallas_call(functools.partial(kernel, n_rows, n_cols), out_shape=(jax....  135 us
    unnamed x2, local copies, waits for them, and re-layouts  3.45 us

profile of v2, /device:TPU:0, one launch (start us, length us, event | category | flops | bytes accessed | tf_op | source)
XLA Modules:
  0.0 143.6 jit_solution(18108756215958206262)
XLA Ops:
  0.6 0.9 convert_reduce_fusion
  1.5 0.7 multiply_add_fusion
  2.2 0.8 select_reduce_fusion
  3.0 0.7 broadcast_in_dim.32
  3.7 135.1 %shard_map.94 = (f32[128,1024]{1,0:T(8,128)}, f32[32,1024]{1,0:T(8,128)}, f32[8,128]{1,0:T(8,128)}) custom-call(f32[1024,1024]{1,0:T(8,128)} %p_ref.1, f32[128,1024]{1,0:T(8,128)} %start_ref.1, f32[1,1024]{1,0:T(1,128)} %bitcast.10, f32[1,1024]{1,0:T(1,128)} %bitcast.11, s32[1,1024]{1,0:T(1,128)} %bitcast.9, f32[4,8,128]{2,1,0:T(8,128)} %bitcast.7), custom_call_target="tpu_custom_call" | custom-call | tf_op jit(solution)/shard_map/pallas_call | solution.py:312
  138.8 0.7 reshape.13
  139.5 0.6 copy.13
  140.1 1.9 %copy.16 = f32[128,1024]{1,0:T(8,128)} copy(f32[128,1024]{1,0:T(8,128)} %get-tuple-element.12) | data formatting | bytes 1048576
  142.0 1.6 %copy.17 = f32[32,1024]{1,0:T(8,128)} copy(f32[32,1024]{1,0:T(8,128)} %get-tuple-element.13) | data formatting | bytes 262144
